TPU v7x, 32 devices: a whole 2x2x4 slice. The times are simulated.
32 devices in a mesh: gr: 8 (over z, x), gc: 4 (over y, core).
Axes of the slice: x: 2, y: 2, z: 4, core: 2. Of those that a mesh axis runs over, the one named last changes fastest.
Arguments:
- orbitals: bfloat16 [1536, 16384], P(None, ('gr', 'gc')), may hold values from -0.046875 to 0.046875
- velocities: bfloat16 [1536, 16384], P(None, ('gr', 'gc')), may hold values from -40 to 40
Outputs:
- new_velocities: float32 [1536, 16384], P(None, ('gr', 'gc'))
- violations: float32 [1], replicated
All inputs are finite; a program needn't handle non-finite values.
Results may differ from a plain program's by a relative error of at most 0.0018.
Values may be sent and summed in bfloat16 or wider, within the bound.
A program may use at most 64 MiB of HBM per device.

v0:
```python
import jax
import jax.numpy as jnp
from jax import lax
from jax.sharding import PartitionSpec as P

M = 1536


def local(orbitals, velocities):
    total_rows = orbitals.shape[0]
    local_cols = orbitals.shape[1]
    row_groups = lax.axis_size("gr")
    edge = total_rows // row_groups
    half = row_groups // 2 + 1
    offsets = jnp.arange(half, dtype=jnp.int32)
    mirror_mask = ((offsets >= 1) & (2 * offsets != row_groups)).astype(jnp.float32)
    orb_blocks = orbitals.reshape(row_groups, edge, local_cols)
    targets = jnp.arange(row_groups, dtype=jnp.int32)
    vel = velocities.astype(jnp.float32)
    vel_b = vel.astype(jnp.bfloat16)
    intersection = jnp.dot(orbitals, vel_b.T, preferred_element_type=jnp.float32)
    sym_local = intersection + intersection.T
    sym_four = sym_local.reshape(row_groups, edge, row_groups, edge)
    every_row = jnp.arange(row_groups, dtype=jnp.int32)
    every_col = (every_row[:, None] + offsets[None, :]) % row_groups
    full_term = sym_four[every_row[:, None], :, every_col, :].reshape(
        row_groups * half * edge, edge
    )
    share_rows = row_groups * half * edge // (row_groups * lax.axis_size("gc"))
    share = lax.psum_scatter(full_term, ("gr", "gc"), scatter_dimension=0, tiled=True)
    rows_here = lax.axis_index(("gr", "gc")) * share_rows + jnp.arange(share_rows, dtype=jnp.int32)
    offset_of = rows_here // edge % half
    weight = jnp.where((offset_of >= 1) & (2 * offset_of != row_groups), 2.0, 1.0)
    local_sq = jnp.sum(weight[:, None] * share * share)
    sym_b = share.astype(jnp.bfloat16)
    joined = lax.all_gather(sym_b, ("gr", "gc"), axis=0, tiled=True)
    piece = joined.reshape(row_groups, half * edge * edge)
    count = piece.shape[0]
    block_rows = jnp.arange(count, dtype=jnp.int32)
    block_cols = (block_rows[:, None] + offsets[None, :]) % row_groups
    blocks = piece.reshape(count, half, edge, edge)
    far_orb = jnp.take(orb_blocks, block_cols, axis=0)
    own_orb = jnp.take(orb_blocks, block_rows, axis=0)
    direct = jnp.einsum("jkab,jkbg->jag", blocks, far_orb, preferred_element_type=jnp.float32)
    mirrored = jnp.einsum("jkab,jag->jkbg", blocks, own_orb, preferred_element_type=jnp.float32)
    row_hot = (block_rows[:, None] == targets[None, :]).astype(jnp.float32)
    col_hot = (block_cols[:, :, None] == targets[None, None, :]).astype(jnp.float32) * mirror_mask[
        None, :, None
    ]
    carry = jnp.einsum("jq,jag->qag", row_hot, direct)
    carry = carry + jnp.einsum("jkq,jkbg->qbg", col_hot, mirrored)
    correction = carry.reshape(total_rows, local_cols)
    summed = lax.psum(local_sq, ("gr", "gc"))
    measured = [jnp.sqrt(summed) / M]
    vel = vel - 0.5 * correction
    return (vel, jnp.stack(measured))


def solution(mesh):
    in_specs = (P(None, ("gr", "gc")), P(None, ("gr", "gc")))
    out_specs = (P(None, ("gr", "gc")), P())
    return jax.shard_map(local, mesh=mesh, in_specs=in_specs, out_specs=out_specs, check_vma=False)
```

profile of v0, /device:TPU:0, one launch (start us, length us, event | category | flops | bytes accessed | tf_op | source)
XLA Modules:
  0.0 295.9 jit_solution(1562498942545767514)
XLA Ops:
  7.2 1.3 copy-done
  8.6 6.4 %fusion.38 = f32[1536,1536]{1,0:T(8,128)} fusion(bf16[1536,512]{1,0:T(8,128)(2,1)S(1)} %copy-done, bf16[1536,512]{1,0:T(8,128)(2,1)} %param.3), kind=kOutput, calls=%fused_computation.61 | convolution fusion | flops 2415919104 | bytes 12582912 | tf_op jit(solution)/shard_map/dot_general | solution.py:21
  15.0 9.6 %copy.20 = f32[1536,1536]{0,1:T(8,128)} copy(f32[1536,1536]{1,0:T(8,128)} %fusion.38) | data formatting | bytes 18874368 | tf_op jit(solution)/shard_map/dot_general | solution.py:21
  24.6 12.1 %bitcast_add_fusion = f32[1536,1536]{1,0:T(8,128)} fusion(f32[1536,1536]{1,0:T(8,128)} %fusion.38, f32[1536,1536]{0,1:T(8,128)} %copy.20), kind=kLoop, calls=%fused_computation.5 | loop fusion | flops 2359296 | bytes 28311552 | tf_op jit(solution)/shard_map/add | solution.py:22
  36.7 12.5 %reshape.135 = f32[8,192,8,192]{3,2,1,0:T(8,128)} reshape(f32[1536,1536]{1,0:T(8,128)} %bitcast_add_fusion) | data formatting | bytes 18874368 | tf_op jit(solution)/shard_map/reshape | solution.py:23
  49.2 12.8 %copy.21 = f32[8,192,8,192]{3,1,2,0:T(8,128)} copy(f32[8,192,8,192]{3,2,1,0:T(8,128)} %reshape.135) | data formatting | bytes 18874368 | tf_op jit(solution)/shard_map/reshape | solution.py:23
  62.0 0.1 reshape.138
  62.1 9.0 %gather_fusion = f32[40,192,192]{2,1,0:T(8,128)} fusion(f32[8,192,8,192]{3,1,2,0:T(8,128)} %copy.21, s32[40]{0:T(128)S(1)} %reshape.138), kind=kCustom, calls=%fused_computation | custom fusion | bytes 11796800 | tf_op jit(solution)/shard_map/gather | solution.py:26
  71.2 125.9 %reduce-scatter.4.cloned.1.call-done = f32[240,192]{1,0:T(8,128)} async-done(((f32[7680,192]{1,0:T(8,128)}), f32[240,192]{1,0:T(8,128)}) %reduce-scatter.4.cloned.1.call-update) | async-done | bytes 184336
  197.2 1.1 copy.35
  198.2 1.3 fusion.19
  199.5 0.1 reshape.146
  199.6 0.1 copy.24
  199.7 5.7 %gather_fusion.1 = bf16[40,192,512]{2,1,0:T(8,128)(2,1)} fusion(bf16[8,192,512]{2,1,0:T(8,128)(2,1)S(1)} %bitcast.39, s32[1024]{0:T(1024)S(1)} %pad_clamp_fusion.1), kind=kCustom, calls=%fused_computation.1 | custom fusion | bytes 15728800 | tf_op jit(solution)/shard_map/jit(_take)/gather | solution.py:42
  205.4 1.8 gather_fusion.2
  207.3 40.2 %psum.7 = f32[]{:T(128)} all-reduce(f32[]{:T(128)} %get-tuple-element.2), channel_id=1, replica_groups=mesh['gr'=8,'gc'=4] {'gr','gc'}, use_global_device_ids=true, to_apply=%region_2.3 | all-reduce | flops 1 | bytes 8 | tf_op jit(solution)/shard_map/psum | solution.py:53
  248.2 10.4 %all-gather.3.cloned.1.call-done = bf16[32,240,192]{1,2,0:T(8,128)(2,1)} async-done(((bf16[1,240,192]{1,2,0:T(8,128)(2,1)}), bf16[32,240,192]{1,2,0:T(8,128)(2,1)}) %all-gather.3.cloned.1.call-update) | async-done | bytes 2949136 | tf_op jit(solution)/shard_map/all_gather | solution.py:36
  258.6 5.7 %copy.23 = bf16[32,240,192]{2,1,0:T(8,128)(2,1)} copy(bf16[32,240,192]{1,2,0:T(8,128)(2,1)} %all-gather.3.cloned.1.call-done) | data formatting | bytes 5898240 | tf_op jit(solution)/shard_map/all_gather | solution.py:36
  264.4 6.4 %fusion.11 = bf16[8,192,512]{2,1,0:T(8,128)(2,1)S(1)} fusion(bf16[8,5,192,192]{3,2,1,0:T(8,128)(2,1)} %bitcast.42, bf16[8,5,192,512]{3,2,1,0:T(8,128)(2,1)} %bitcast.44, pred[8,5]{1,0:T(8,128)(4,1)S(1)} %copy.24), kind=kOutput, calls=%fused_computation.15 | convolution fusion | flops 1513881600 | bytes 12386344 | tf_op jit(solution)/shard_map/jkab,jkbg->jag/dot_general | solution.py:44
  270.8 2.7 fusion.7
  273.5 3.8 %fusion.14 = bf16[8,5,192,512]{3,2,1,0:T(8,128)(2,1)S(1)} fusion(bf16[8,5,192,192]{3,2,1,0:T(8,128)(2,1)S(1)} %bitcast.43, bf16[8,192,512]{2,1,0:T(8,128)(2,1)} %gather_fusion.2, pred[8]{0:T(512)(128)(4,1)S(1)} %iota_compare_fusion.3), kind=kOutput, calls=%fused_computation.16 | convolution fusion | flops 1510735872 | bytes 12386312 | tf_op jit(solution)/shard_map/jkab,jag->jkbg/dot_general | solution.py:45
  277.3 6.6 %fusion.6 = f32[8,192,512]{2,0,1:T(8,128)S(1)} fusion(f32[8,192,512]{2,0,1:T(8,128)} %fusion.7, bf16[8,5,192,512]{3,2,1,0:T(8,128)(2,1)S(1)} %fusion.14, bf16[5]{0:T(256)(128)(2,1)S(1)} %and_convert_fusion, s32[8,5]{0,1:T(8,128)S(1)} %add_select_fusion), kind=kOutput, calls=%fused_computation.12 | convolution fusion | flops 64488064 | bytes 14155946 | tf_op jit(solution)/shard_map/jkq,jkbg->qbg/dot_general | solution.py:51
  283.9 1.8 copy.28
  285.8 2.2 bitcast_subtract_fusion
  (19 shorter events, 0.2 us)
Async XLA Ops:
  7.2 1.4 copy-start
  7.2 190.0 %reduce-scatter.4.cloned.1.call-start = ((), (), s32[]{:S(2)}) async-start(), calls=%async_computation.2 | async-start | bytes 8110080
  71.1 187.5 %all-gather.3.cloned.1.call-start = ((), (), s32[]{:S(2)}) async-start(), calls=%async_computation.1 | async-start | bytes 3244032 | tf_op jit(solution)/shard_map/all_gather | solution.py:36
  270.8 2.7 copy-start.1
  283.9 1.8 copy-start.2
Sparse Core Ops, SparseCore 0:
  71.3 125.8 reduce-scatter.3
  200.6 57.9 all-gather.2
where the time goes:
time: 297 us; the launch traced here: 296 us
  waiting for transfers between devices  136 us (46%)
  local copies, waits for them, and re-layouts  61.7 us (21%)
  blocking collectives  40.2 us (14%)
  matrix products  25.9 us (9%)
  between operations  16 us (5%)
  other arithmetic  15.6 us (5%)
    unnamed x3, waiting for transfers between devices  126 us
    psum x1, blocking collectives, local(): summed = lax.psum(local_sq, ('gr', 'gc'))  40.2 us
    reshape x2, local copies, waits for them, and re-layouts, local(): sym_four = sym_local.reshape(row_groups, edge, row_groups, edge)  25.3 us
    add x1, other arithmetic, local(): sym_local = intersection + intersection.T  12.1 us
    all_gather x1, waiting for transfers between devices, local(): joined = lax.all_gather(sym_b, ('gr', 'gc'), axis=0, tiled=True)  10.4 us
    dot_general x1, local copies, waits for them, and re-layouts, local(): jnp.dot(orbitals, vel_b.T, preferred_element_type=jnp.float32)  9.62 us
    gather x1, local copies, waits for them, and re-layouts, local(): sym_four[every_row[:, None], :, every_col, :]  9.02 us
    dot_general x1, matrix products, local(): carry = carry + jnp.einsum('jkq,jkbg->qbg', col_hot, mirrored)  6.63 us
  transfers between devices with their start and end apart: 2, of which 2 were waited for; matrix products, arithmetic and copies ran while one was open for 3% of the time, Pallas kernels for 0%

commit v1 on v0

v1 whole, which is shorter than its diff:
```python
import functools

import jax
import jax.numpy as jnp
from jax import lax
from jax.experimental import pallas as pl
from jax.experimental.pallas import tpu as pltpu
from jax.sharding import PartitionSpec as P

MESH = pl.DeviceIdType.MESH
T = 128
ROWS = 16
LANES = 3


def packed_blocks(count):
    blocks = [(i, i) for i in range(count)]
    return blocks + [(i, j) for i in range(count) for j in range(i + 1, count)]


def bits_of(size):
    return size.bit_length() - 1


def stages(gr, gc, n_gr, n_gc):
    def axis_bits(at, size, low):
        found = []
        here = (at // 2**low) % 2
        low_partner = at + (1 - 2 * here) * 2**low
        if low == 0:
            found.append((low_partner, here))
        top = bits_of(size) - 1
        values = [(at // 2**k) % 2 for k in range(top + 1)]
        for k in range(1, top + 1):
            above = values[k + 1] if k < top else 0
            gray = values[k] + above - 2 * values[k] * above
            partner = at
            for m in range(1, k + 1):
                partner = partner + (1 - 2 * values[m]) * 2**m
            found.append((partner, gray))
        return found

    in_gc = [((gr, p), v) for p, v in axis_bits(gc, n_gc, 0)]
    in_gr = [((p, gc), v) for p, v in axis_bits(gr, n_gr, 0)]
    return in_gc[:1], in_gc[1:] + in_gr


def kernel(n_gr, n_gc, lanes, orb, vel, sym, square, left, right, acc, out_buf, in_buf, whole, send_sem, recv_sem):
    gr, gc = lax.axis_index("gr"), lax.axis_index("gc")
    first, rest = stages(gr, gc, n_gr, n_gc)
    every = first + rest
    depth = len(every)
    count = orb.shape[0] // T
    blocks = packed_blocks(count)
    slot = {pair: at for at, pair in enumerate(blocks)}

    barrier = pltpu.get_barrier_semaphore()
    for partner, _ in every:
        pl.semaphore_signal(barrier, inc=1, device_id=partner, device_id_type=MESH)

    half = orb.shape[1]
    left[:, :half] = orb[...]
    left[:, half:] = vel[...]
    right[:, :half] = vel[...]
    right[:, half:] = orb[...]
    used = len(blocks) * T
    if acc.shape[0] > used:
        acc[used:, :] = jnp.zeros((acc.shape[0] - used, T), jnp.float32)

    for i in range(count):
        strip = lax.dot_general(
            left[i * T : (i + 1) * T, :],
            right[i * T :, :],
            (((1,), (1,)), ((), ())),
            preferred_element_type=jnp.float32,
        )
        for j in range(i, count):
            at = slot[(i, j)] * T
            acc[at : at + T, :] = strip[:, (j - i) * T : (j - i + 1) * T]

    pl.semaphore_wait(barrier, depth)

    def rows(start, size):
        return pl.ds(pl.multiple_of(start, ROWS), size)

    orders = []
    for lane in range(len(lanes)):
        turn = lane * len(rest) // len(lanes)
        orders.append(first + rest[turn:] + rest[:turn])
    at = [base for base, _ in lanes]
    sends = []

    def reduce_start(lane, step):
        base, size = lanes[lane]
        partner, value = orders[lane][step]
        size = size >> (step + 1)
        away = at[lane] + (1 - value) * size
        at[lane] = at[lane] + value * size
        landing = base + (lanes[lane][1] - 2 * size)
        out_buf[rows(away, size), :] = acc[rows(away, size), :].astype(jnp.bfloat16)
        copy = pltpu.make_async_remote_copy(
            src_ref=out_buf.at[rows(away, size), :],
            dst_ref=in_buf.at[pl.ds(landing, size), :],
            send_sem=send_sem.at[lane, step],
            recv_sem=recv_sem.at[lane, step],
            device_id=partner,
            device_id_type=MESH,
        )
        copy.start()
        sends.append(copy)
        return copy, landing, size

    flying = [reduce_start(lane, 0) for lane in range(len(lanes))]
    for step in range(depth):
        for lane in range(len(lanes)):
            copy, landing, size = flying[lane]
            copy.wait_recv()
            here = rows(at[lane], size)
            total = acc[here, :] + in_buf[landing : landing + size, :].astype(jnp.float32)
            if step + 1 < depth:
                acc[here, :] = total
                flying[lane] = reduce_start(lane, step + 1)
            else:
                whole[here, :] = total.astype(jnp.bfloat16)

    def gather_start(lane, step):
        base, size = lanes[lane]
        partner, value = orders[lane][step]
        size = size >> (step + 1)
        mine = rows(at[lane], size)
        at[lane] = at[lane] - value * size
        copy = pltpu.make_async_remote_copy(
            src_ref=whole.at[mine, :],
            dst_ref=whole.at[mine, :],
            send_sem=send_sem.at[lane, depth + step],
            recv_sem=recv_sem.at[lane, depth + step],
            device_id=partner,
            device_id_type=MESH,
        )
        copy.start()
        sends.append(copy)
        return copy

    flying = [gather_start(lane, depth - 1) for lane in range(len(lanes))]
    for step in range(depth - 2, -2, -1):
        for lane in range(len(lanes)):
            flying[lane].wait_recv()
            if step >= 0:
                flying[lane] = gather_start(lane, step)

    total = jnp.zeros((8, T), jnp.float32)
    for at_slot, (i, j) in enumerate(blocks):
        block = whole[at_slot * T : (at_slot + 1) * T, :]
        value = block.astype(jnp.float32)
        weight = 1.0 if i == j else 2.0
        total = total + weight * jnp.sum((value * value).reshape(T // 8, 8, T), axis=0)
        sym[i * T : (i + 1) * T, j * T : (j + 1) * T] = block
        if i != j:
            sym[j * T : (j + 1) * T, i * T : (i + 1) * T] = block.T
    square[...] = total
    for copy in sends:
        copy.wait_send()


def solution(mesh):
    n_gr, n_gc = mesh.shape["gr"], mesh.shape["gc"]
    devices = n_gr * n_gc

    def local(orbitals, velocities):
        total_rows, cols = orbitals.shape
        count = total_rows // T
        unit = ROWS * devices
        units = -(-(count * (count + 1) // 2 * T) // unit)
        lanes, base = [], 0
        for lane in range(LANES):
            size = (units * (lane + 1) // LANES - units * lane // LANES) * unit
            lanes.append((base, size))
            base += size
        depth = bits_of(devices)
        vmem = pl.BlockSpec(memory_space=pltpu.VMEM)
        sym, square = pl.pallas_call(
            functools.partial(kernel, n_gr, n_gc, lanes),
            out_shape=(
                jax.ShapeDtypeStruct((total_rows, total_rows), jnp.bfloat16),
                jax.ShapeDtypeStruct((8, T), jnp.float32),
            ),
            in_specs=[vmem, vmem],
            out_specs=(vmem, vmem),
            scratch_shapes=[
                pltpu.VMEM((total_rows, 2 * cols), jnp.bfloat16),
                pltpu.VMEM((total_rows, 2 * cols), jnp.bfloat16),
                pltpu.VMEM((base, T), jnp.float32),
                pltpu.VMEM((base, T), jnp.bfloat16),
                pltpu.VMEM((base, T), jnp.bfloat16),
                pltpu.VMEM((base, T), jnp.bfloat16),
                pltpu.SemaphoreType.DMA((LANES, 2 * depth)),
                pltpu.SemaphoreType.DMA((LANES, 2 * depth)),
            ],
            compiler_params=pltpu.CompilerParams(
                collective_id=0, has_side_effects=True, vmem_limit_bytes=60 * 2**20
            ),
        )(orbitals, velocities)
        violation = jnp.sqrt(jnp.sum(square)) / total_rows
        moved = jnp.dot(sym, orbitals, preferred_element_type=jnp.float32)
        return velocities.astype(jnp.float32) - 0.5 * moved, violation[None]

    spec = P(None, ("gr", "gc"))
    return jax.shard_map(
        local, mesh=mesh, in_specs=(spec, spec), out_specs=(spec, P()), check_vma=False
    )
```

time: 297 us -> 71.9 us (0.24)
  the two profiles are of different devices: /device:TPU:0 before, /device:TPU:21 now
where the time goes in v1:
time: 71.9 us; the launch traced here: 71.7 us
  Pallas kernels  61.3 us (85%)
  matrix products  6.62 us (9%)
  between operations  2.49 us (3%)
  other arithmetic  1.29 us (2%)
    pallas_call x1, Pallas kernels, local(): pl.pallas_call(functools.partial(kernel, n_gr, n_gc, lanes), out_shape=(j...  61.3 us
    dot_general x1, matrix products, local(): moved = jnp.dot(sym, orbitals, preferred_element_type=jnp.float32)  6.62 us

profile of v1, /device:TPU:21, one launch (start us, length us, event | category | flops | bytes accessed | tf_op | source)
XLA Modules:
  0.0 71.7 jit_solution(2983984540169531251)
XLA Ops:
  0.6 0.0 copy-start.1
  0.6 0.0 copy-start
  0.6 61.3 %shard_map.41 = (bf16[1536,1536]{1,0:T(8,128)(2,1)}, f32[8,128]{1,0:T(8,128)}) custom-call(bf16[1536,512]{1,0:T(8,128)(2,1)} %orb.1, bf16[1536,512]{1,0:T(8,128)(2,1)} %vel.1), custom_call_target="tpu_custom_call" | custom-call | tf_op jit(solution)/shard_map/pallas_call | solution.py:181
  62.0 1.3 %reduce_sum.9 = f32[]{:T(128)} reduce(f32[8,128]{1,0:T(8,128)} %get-tuple-element.5, f32[]{:T(128)} %constant.2.clone.1), dimensions={0,1}, to_apply=%region_0.0 | reduce | flops 1023 | bytes 4104 | tf_op jit(solution)/shard_map/reduce_sum | solution.py:203
  64.0 0.0 copy-done.1
  64.0 0.0 copy-done
  64.0 6.6 %fusion = f32[1536,512]{1,0:T(8,128)} fusion(bf16[1536,1536]{1,0:T(8,128)(2,1)} %get-tuple-element.4, bf16[1536,512]{1,0:T(8,128)(2,1)S(1)} %copy-done, bf16[1536,512]{1,0:T(8,128)(2,1)S(1)} %copy-done.1), kind=kOutput, calls=%fused_computation.1 | convolution fusion | flops 2418278400 | bytes 11010048 | tf_op jit(solution)/shard_map/dot_general | solution.py:204
Async XLA Ops:
  0.6 63.3 %copy-start.1 = (bf16[1536,512]{1,0:T(8,128)(2,1)S(1)}, bf16[1536,512]{1,0:T(8,128)(2,1)}, u32[]{:S(2)}) copy-start(bf16[1536,512]{1,0:T(8,128)(2,1)} %vel.1) | copy-start | bytes 4718596
  0.6 63.3 %copy-start = (bf16[1536,512]{1,0:T(8,128)(2,1)S(1)}, bf16[1536,512]{1,0:T(8,128)(2,1)}, u32[]{:S(2)}) copy-start(bf16[1536,512]{1,0:T(8,128)(2,1)} %orb.1) | copy-start | bytes 4718596

commit v2 on v1

v2 whole, which is shorter than its diff:
```python
import functools

import jax
import jax.numpy as jnp
from jax import lax
from jax.experimental import pallas as pl
from jax.experimental.pallas import tpu as pltpu
from jax.sharding import PartitionSpec as P

MESH = pl.DeviceIdType.MESH
T = 128
ROWS = 16
BATCHES = 2
WEIGHTS = (3, 3, 4, 0)


def packed_blocks(count):
    return [(i, j) for i in range(count) for j in range(i, count)]


def bits_of(size):
    return size.bit_length() - 1


def stages(gr, gc, n_gr, n_gc):
    def axis_bits(at, size, low):
        found = []
        here = (at // 2**low) % 2
        low_partner = at + (1 - 2 * here) * 2**low
        if low == 0:
            found.append((low_partner, here))
        top = bits_of(size) - 1
        values = [(at // 2**k) % 2 for k in range(top + 1)]
        for k in range(1, top + 1):
            above = values[k + 1] if k < top else 0
            gray = values[k] + above - 2 * values[k] * above
            partner = at
            for m in range(1, k + 1):
                partner = partner + (1 - 2 * values[m]) * 2**m
            found.append((partner, gray))
        return found

    in_gc = [((gr, p), v) for p, v in axis_bits(gc, n_gc, 0)]
    in_gr = [((p, gc), v) for p, v in axis_bits(gr, n_gr, 0)]
    return in_gc[:1], in_gc[1:] + in_gr


def lane_orders(first, rest):
    early, last = rest[:-1], rest[-1:]
    orders = []
    for lane in range(len(WEIGHTS) - 1):
        turn = lane % len(early)
        orders.append(first + early[turn:] + early[:turn] + last)
    return orders + [first + last + early]


def kernel(
    n_gr, n_gc, lanes, orb, vel, new, norm,
    left, right, acc, out_buf, in_buf, whole, sym, send_sem, recv_sem,
):
    gr, gc = lax.axis_index("gr"), lax.axis_index("gc")
    first, rest = stages(gr, gc, n_gr, n_gc)
    every = first + rest
    depth = len(every)
    count = orb.shape[0] // T
    blocks = packed_blocks(count)
    slot = {pair: at for at, pair in enumerate(blocks)}
    used = len(blocks) * T

    barrier = pltpu.get_barrier_semaphore()
    for partner, _ in every:
        pl.semaphore_signal(barrier, inc=1, device_id=partner, device_id_type=MESH)

    half = orb.shape[1]
    left[:, :half] = orb[...]
    left[:, half:] = vel[...]
    right[:, :half] = vel[...]
    right[:, half:] = orb[...]
    if acc.shape[0] > used:
        acc[used:, :] = jnp.zeros((acc.shape[0] - used, T), jnp.float32)

    def rows(start, size):
        return pl.ds(pl.multiple_of(start, ROWS), size)

    by_kind = lane_orders(first, rest)
    orders = [by_kind[kind] for _, _, kind in lanes]
    at = [base for base, _, _ in lanes]
    sends = []
    flying = [None] * len(lanes)

    def reduce_start(lane, step):
        base, length, _ = lanes[lane]
        partner, value = orders[lane][step]
        size = length >> (step + 1)
        away = rows(at[lane] + (1 - value) * size, size)
        at[lane] = at[lane] + value * size
        landing = base + (length - 2 * size)
        out_buf[away, :] = acc[away, :].astype(jnp.bfloat16)
        copy = pltpu.make_async_remote_copy(
            src_ref=out_buf.at[away, :],
            dst_ref=in_buf.at[pl.ds(landing, size), :],
            send_sem=send_sem.at[lane, step],
            recv_sem=recv_sem.at[lane, step],
            device_id=partner,
            device_id_type=MESH,
        )
        copy.start()
        sends.append(copy)
        flying[lane] = (copy, landing, size)

    started = 0
    for i in range(count):
        strip = lax.dot_general(
            left[i * T : (i + 1) * T, :],
            right[i * T :, :],
            (((1,), (1,)), ((), ())),
            preferred_element_type=jnp.float32,
        )
        for j in range(i, count):
            here = slot[(i, j)] * T
            acc[here : here + T, :] = strip[:, (j - i) * T : (j - i + 1) * T]
        done = (slot[(i, count - 1)] + 1) * T if i + 1 < count else acc.shape[0]
        while started < len(lanes) and lanes[started][0] + lanes[started][1] <= done:
            if started == 0:
                pl.semaphore_wait(barrier, depth)
            reduce_start(started, 0)
            started += 1

    for step in range(depth):
        for lane in range(len(lanes)):
            copy, landing, size = flying[lane]
            copy.wait_recv()
            here = rows(at[lane], size)
            total = acc[here, :] + in_buf[landing : landing + size, :].astype(jnp.float32)
            if step + 1 < depth:
                acc[here, :] = total
                reduce_start(lane, step + 1)
            else:
                whole[here, :] = total.astype(jnp.bfloat16)

    def gather_start(lane, step):
        _, length, _ = lanes[lane]
        partner, value = orders[lane][step]
        size = length >> (step + 1)
        mine = rows(at[lane], size)
        at[lane] = at[lane] - value * size
        copy = pltpu.make_async_remote_copy(
            src_ref=whole.at[mine, :],
            dst_ref=whole.at[mine, :],
            send_sem=send_sem.at[lane, depth + step],
            recv_sem=recv_sem.at[lane, depth + step],
            device_id=partner,
            device_id_type=MESH,
        )
        copy.start()
        sends.append(copy)
        flying[lane] = copy

    for lane in range(len(lanes)):
        gather_start(lane, depth - 1)
    for step in range(depth - 2, -1, -1):
        for lane in range(len(lanes)):
            flying[lane].wait_recv()
            gather_start(lane, step)

    square = jnp.zeros((8, T), jnp.float32)
    unpacked = 0
    for lane, (base, length, _) in enumerate(lanes):
        flying[lane].wait_recv()
        while unpacked < len(blocks) and (unpacked + 1) * T <= base + length:
            i, j = blocks[unpacked]
            block = whole[unpacked * T : (unpacked + 1) * T, :]
            value = block.astype(jnp.float32)
            part = jnp.sum((value * value).reshape(T // 8, 8, T), axis=0)
            square = square + (part if i == j else 2.0 * part)
            sym[i * T : (i + 1) * T, j * T : (j + 1) * T] = block
            if i != j:
                sym[j * T : (j + 1) * T, i * T : (i + 1) * T] = block.T
            unpacked += 1
            if j + 1 == count and i % 2 == 1 or unpacked == len(blocks):
                strip = slice(i // 2 * 2 * T, (i + 1) * T)
                moved = jnp.dot(sym[strip, :], orb[...], preferred_element_type=jnp.float32)
                new[strip, :] = vel[strip, :].astype(jnp.float32) - 0.5 * moved
    norm[0] = jnp.sqrt(jnp.sum(square)) / orb.shape[0]
    for copy in sends:
        copy.wait_send()


def solution(mesh):
    n_gr, n_gc = mesh.shape["gr"], mesh.shape["gc"]
    devices = n_gr * n_gc

    def local(orbitals, velocities):
        total_rows, cols = orbitals.shape
        count = total_rows // T
        unit = ROWS * devices
        units = -(-(count * (count + 1) // 2 * T) // unit)
        weights = WEIGHTS * BATCHES
        lanes, base, given = [], 0, 0
        for lane, weight in enumerate(weights):
            given += weight
            size = units * given // sum(weights) * unit - base
            if size:
                lanes.append((base, size, lane % len(WEIGHTS)))
            base += size
        depth = bits_of(devices)
        vmem = pl.BlockSpec(memory_space=pltpu.VMEM)
        return pl.pallas_call(
            functools.partial(kernel, n_gr, n_gc, lanes),
            out_shape=(
                jax.ShapeDtypeStruct((total_rows, cols), jnp.float32),
                jax.ShapeDtypeStruct((1,), jnp.float32),
            ),
            in_specs=[vmem, vmem],
            out_specs=(vmem, pl.BlockSpec(memory_space=pltpu.SMEM)),
            scratch_shapes=[
                pltpu.VMEM((total_rows, 2 * cols), jnp.bfloat16),
                pltpu.VMEM((total_rows, 2 * cols), jnp.bfloat16),
                pltpu.VMEM((base, T), jnp.float32),
                pltpu.VMEM((base, T), jnp.bfloat16),
                pltpu.VMEM((base, T), jnp.bfloat16),
                pltpu.VMEM((base, T), jnp.bfloat16),
                pltpu.VMEM((total_rows, total_rows), jnp.bfloat16),
                pltpu.SemaphoreType.DMA((len(lanes), 2 * depth)),
                pltpu.SemaphoreType.DMA((len(lanes), 2 * depth)),
            ],
            compiler_params=pltpu.CompilerParams(
                collective_id=0, has_side_effects=True, vmem_limit_bytes=34 * 2**20
            ),
        )(orbitals, velocities)

    spec = P(None, ("gr", "gc"))
    return jax.shard_map(
        local, mesh=mesh, in_specs=(spec, spec), out_specs=(spec, P()), check_vma=False
    )
```

time: 71.9 us -> 57.2 us (0.80)
  the two profiles are of different devices: /device:TPU:21 before, /device:TPU:0 now
where the time goes in v2:
time: 57.2 us; the launch traced here: 57 us
  Pallas kernels  50.1 us (88%)
  local copies, waits for them, and re-layouts  4.48 us (8%)
  between operations  2.41 us (4%)
    pallas_call x1, Pallas kernels, local(): pl.pallas_call(functools.partial(kernel, n_gr, n_gc, lanes), out_shape=(j...  50.1 us
    unnamed x5, local copies, waits for them, and re-layouts  4.48 us

profile of v2, /device:TPU:0, one launch (start us, length us, event | category | flops | bytes accessed | tf_op | source)
XLA Modules:
  0.0 57.0 jit_solution(14208250977481310353)
XLA Ops:
  0.6 0.0 copy-start
  0.6 1.4 %copy-done = bf16[1536,512]{1,0:T(8,128)(2,1)S(1)} copy-done((bf16[1536,512]{1,0:T(8,128)(2,1)S(1)}, bf16[1536,512]{1,0:T(8,128)(2,1)}, u32[]{:S(2)}) %copy-start) | copy-done | bytes 1572888
  2.0 0.0 copy-start.1
  2.0 1.4 %copy-done.1 = bf16[1536,512]{1,0:T(8,128)(2,1)S(1)} copy-done((bf16[1536,512]{1,0:T(8,128)(2,1)S(1)}, bf16[1536,512]{1,0:T(8,128)(2,1)}, u32[]{:S(2)}) %copy-start.1) | copy-done | bytes 1572888
  3.4 50.1 %shard_map.41 = (f32[1536,512]{1,0:T(8,128)S(1)}, f32[1]{0:T(128)}) custom-call(bf16[1536,512]{1,0:T(8,128)(2,1)S(1)} %copy-done, bf16[1536,512]{1,0:T(8,128)(2,1)S(1)} %copy-done.1), custom_call_target="tpu_custom_call" | custom-call | tf_op jit(solution)/shard_map/pallas_call | solution.py:208
  53.6 1.7 %copy.6 = f32[1536,512]{1,0:T(8,128)} copy(f32[1536,512]{1,0:T(8,128)S(1)} %get-tuple-element.4) | data formatting | bytes 6291456
Async XLA Ops:
  0.6 1.4 %copy-start = (bf16[1536,512]{1,0:T(8,128)(2,1)S(1)}, bf16[1536,512]{1,0:T(8,128)(2,1)}, u32[]{:S(2)}) copy-start(bf16[1536,512]{1,0:T(8,128)(2,1)} %orb.1) | copy-start | bytes 4718596
  2.0 1.4 %copy-start.1 = (bf16[1536,512]{1,0:T(8,128)(2,1)S(1)}, bf16[1536,512]{1,0:T(8,128)(2,1)}, u32[]{:S(2)}) copy-start(bf16[1536,512]{1,0:T(8,128)(2,1)} %vel.1) | copy-start | bytes 4718596
